TPU v7x, 512 devices: a whole 4x4x16 slice. The times are simulated.
512 devices in a mesh: edp: 32 (over z_hi, y, core), etp: 16 (over z_lo, x).
Axes of the slice: x: 4, y: 4, z: 16 (z_hi: 4, z_lo: 4; z = z_hi * 4 + z_lo), core: 2. Of those that a mesh axis runs over, the one named last changes fastest.
Arguments:
- tokens: bfloat16 [16384, 3072], P('edp'), may hold values from -6 to 6
- expert_ids: int32 [16384, 2], P('edp'), may hold values from 0 to 7, as said below
- route_weight: float32 [16384, 2], P('edp'), may hold values from 0.2 to 1
- index_list: int32 [32, 256], P('edp'), may hold values from 0 to 512, as said below
- gate_weight: bfloat16 [3072, 8192], P('edp', 'etp'), may hold values from -0.109375 to 0.109375
- up_weight: bfloat16 [3072, 8192], P('edp', 'etp'), may hold values from -0.109375 to 0.109375
- down_weight: bfloat16 [8192, 3072], P('etp', 'edp'), may hold values from -0.0625 to 0.0625
Outputs:
- expert_out: bfloat16 [16384, 3072], P(('edp', 'etp'))
Inputs may be any that keep to these rules, and one draw needn't show every extreme that they name: `index_list`: row b lists, increasing, the positions within block b of the tokens that name expert 0, then 512 in the remaining slots; in every draw some block is full. `expert_ids`: each token names two different experts; a token names expert 0 exactly when its position stands in its block's row of index_list.
All inputs are finite; a program needn't handle non-finite values.
Results may differ from a plain program's by a relative error of at most 0.018.
Values may be sent and summed in bfloat16 or wider, within the bound.
No kernel may reach another device: no remote copies, remote signals or barrier semaphores. Data moves between devices by JAX's collectives and lax.ppermute only.
A program may use at most 64 MiB of HBM per device.

v0:
```python
import jax
import jax.numpy as jnp
from jax import lax
from jax.sharding import PartitionSpec as P


def gather_turned(arrays, axis, dims):
    turned = [jnp.moveaxis(a, dim, 0) for a, dim in zip(arrays, dims)]
    widths = [t[0].size for t in turned]
    both = jnp.concatenate([t.reshape(-1, w) for t, w in zip(turned, widths)], axis=1)
    result = lax.all_gather(both, axis, axis=0, tiled=True)
    blocks = jnp.split(result, [sum(widths[:k]) for k in range(1, len(widths))], axis=1)
    return tuple(
        (
            jnp.moveaxis(b.reshape(-1, *t.shape[1:]), 0, dim)
            for b, t, dim in zip(blocks, turned, dims)
        )
    )


def in_blocks(value, dim, devices):
    before, after = (value.shape[:dim], value.shape[dim + 1 :])
    return jnp.moveaxis(value.reshape(*before, devices, -1, *after), dim, 0)


def sum_at_owner(value, axis, dim):
    devices = lax.axis_size(axis)
    blocks = lax.all_to_all(in_blocks(value, dim, devices), axis, 0, 0, tiled=True)
    return jnp.sum(blocks.astype(jnp.float32), axis=0)


def shards(tokens, expert_ids, route_weight, index_list, gate_weight, up_weight, down_weight):
    block_rows = tokens.shape[0]
    slot_rows = index_list[0]
    combine = jnp.sum(
        jnp.where(expert_ids == 0, route_weight, jnp.zeros_like(route_weight)), axis=1
    )
    is_live = slot_rows < block_rows
    safe_rows = jnp.minimum(slot_rows, block_rows - 1)
    inputs = jnp.take(tokens, safe_rows, axis=0)
    row_scale = jnp.where(is_live, jnp.take(combine, safe_rows), jnp.zeros_like(combine[:1]))
    gate_full, up_full, down_full = gather_turned(
        (gate_weight, up_weight, down_weight), "edp", (0, 0, 1)
    )
    gate_sum = jnp.dot(inputs, gate_full, preferred_element_type=jnp.float32)
    up_sum = jnp.dot(inputs, up_full, preferred_element_type=jnp.float32)
    hidden = (jax.nn.silu(gate_sum) * up_sum * row_scale[:, None]).astype(jnp.bfloat16)
    partial_terms = jnp.dot(hidden, down_full, preferred_element_type=jnp.float32)
    placing = (jnp.arange(block_rows)[:, None] == slot_rows[None, :]).astype(jnp.float32)
    partial_terms = jnp.dot(placing, partial_terms, preferred_element_type=jnp.float32)
    shares = sum_at_owner(partial_terms.astype(jnp.bfloat16), "etp", 0)
    return shares.astype(jnp.bfloat16)


def solution(mesh):
    in_specs = (
        P("edp", None),
        P("edp", None),
        P("edp", None),
        P("edp", None),
        P("edp", "etp"),
        P("edp", "etp"),
        P("etp", "edp"),
    )
    out_specs = P(("edp", "etp"), None)
    return jax.shard_map(shards, mesh=mesh, in_specs=in_specs, out_specs=out_specs, check_vma=False)
```

profile of v0, /device:TPU:16, one launch (start us, length us, event | category | flops | bytes accessed | tf_op | source)
XLA Modules:
  0.0 259.0 jit_solution(4967588532074355939)
XLA Ops:
  6.5 0.0 copy-start
  6.5 0.0 all-gather.2.cloned.1.call-start
  6.5 1.9 pad_maximum_fusion
  8.4 0.0 all-gather.2.cloned.1.call-update
  8.4 0.7 compare_select_fusion.1
  9.1 0.7 fusion.18
  9.9 1.9 gather_fusion.1
  11.8 0.0 copy-done
  11.8 0.0 copy-start.2
  11.8 2.7 %gather_fusion = bf16[256,3072]{1,0:T(8,128)(2,1)} fusion(bf16[512,3072]{1,0:T(8,128)(2,1)S(1)} %copy-done, s32[1024]{0:T(1024)S(1)} %pad_clamp_fusion), kind=kCustom, calls=%fused_computation | custom fusion | bytes 3146752 | tf_op jit(solution)/shard_map/jit(_take)/gather | solution.py:40
  14.6 0.0 copy-done.2
  14.6 146.0 %all-gather.2.cloned.1.call-done = bf16[3072,1536]{1,0:T(8,128)(2,1)} async-done(((bf16[96,1536]{1,0:T(8,128)(2,1)}), bf16[3072,1536]{1,0:T(8,128)(2,1)}) %all-gather.2.cloned.1.call-update) | async-done | bytes 9437200 | tf_op jit(solution)/shard_map/all_gather | solution.py:11
  160.6 0.0 copy-start.1
  160.6 3.5 %fusion.4 = f32[256,512]{1,0:T(8,128)S(1)} fusion(bf16[3072,1536]{1,0:T(8,128)(2,1)} %all-gather.2.cloned.1.call-done, bf16[256,3072]{1,0:T(8,128)(2,1)} %gather_fusion, pred[256]{0:T(512)(128)(4,1)S(1)} %compare_and_fusion), kind=kOutput, calls=%fused_computation.7 | convolution fusion | flops 806092800 | bytes 5243136 | tf_op jit(solution)/shard_map/dot_general | solution.py:45
  164.1 0.0 copy-done.1
  164.1 2.9 %fusion.14 = bf16[256,512]{1,0:T(8,128)(2,1)S(1)} fusion(bf16[3072,1536]{1,0:T(8,128)(2,1)} %all-gather.2.cloned.1.call-done, bf16[256,3072]{1,0:T(8,128)(2,1)S(1)} %copy-done.1, pred[256]{0:T(512)(128)(4,1)S(1)} %compare_and_fusion, f32[256,512]{1,0:T(8,128)S(1)} %fusion.4, f32[256]{0:T(256)S(1)} %compare_select_fusion.3), kind=kOutput, calls=%fused_computation.12 | convolution fusion | flops 807010304 | bytes 5506304 | tf_op jit(solution)/shard_map/dot_general | solution.py:46
  167.0 5.4 %convolution_convert_fusion = bf16[512,3072]{1,0:T(8,128)(2,1)} fusion(bf16[256,512]{1,0:T(8,128)(2,1)S(1)} %fusion.14, bf16[3072,1536]{1,0:T(8,128)(2,1)} %all-gather.2.cloned.1.call-done, s32[256]{0:T(256)S(1)} %bitcast.11), kind=kOutput, calls=%fused_computation.2 | convolution fusion | flops 1612316672 | bytes 6554624 | tf_op jit(solution)/shard_map/dot_general | solution.py:50
  172.4 76.6 %all_to_all.5 = bf16[16,32,3072]{2,1,0:T(8,128)(2,1)} all-to-all(bf16[16,32,3072]{2,1,0:T(8,128)(2,1)} %bitcast.7), channel_id=1, replica_groups=mesh['edp'=32,'etp'=16] {'etp'}, dimensions={0} | all-to-all | bytes 6291456 | tf_op jit(solution)/shard_map/all_to_all | solution.py:28
  249.0 3.2 %reduce_sum.22 = bf16[32,3072]{1,0:T(8,128)(2,1)} reduce(bf16[16,32,3072]{2,1,0:T(8,128)(2,1)} %all_to_all.5, bf16[]{:T(256)} %constant.41.clone.1), dimensions={0}, to_apply=%region_1.2 | reduce | flops 1474560 | bytes 3342338 | tf_op jit(solution)/shard_map/reduce_sum | solution.py:29
  (3 shorter events, 0.0 us)
Async XLA Ops:
  6.5 5.3 %copy-start = (bf16[512,3072]{1,0:T(8,128)(2,1)S(1)}, bf16[512,3072]{1,0:T(8,128)(2,1)}, u32[]{:S(2)}) copy-start(bf16[512,3072]{1,0:T(8,128)(2,1)} %param.7) | copy-start | bytes 9437188
  6.5 154.0 %all-gather.2.cloned.1.call-start = ((), (), s32[]{:S(2)}) async-start(), calls=%async_computation.1 | async-start | bytes 9732096 | tf_op jit(solution)/shard_map/all_gather | solution.py:11
  11.8 2.8 %copy-start.2 = (s32[1,256]{1,0:T(1,128)S(1)}, s32[1,256]{1,0:T(1,128)}, u32[]{:S(2)}) copy-start(s32[1,256]{1,0:T(1,128)} %param.10) | copy-start | bytes 3076
  160.6 3.5 %copy-start.1 = (bf16[256,3072]{1,0:T(8,128)(2,1)S(1)}, bf16[256,3072]{1,0:T(8,128)(2,1)}, u32[]{:S(2)}) copy-start(bf16[256,3072]{1,0:T(8,128)(2,1)} %gather_fusion) | copy-start | bytes 4718596
Sparse Core Ops, SparseCore 0:
  10.5 150.0 all-gather.1
where the time goes:
time: 259 us
  waiting for transfers between devices  146 us (56%)
  blocking collectives  76.6 us (30%)
  between operations  13.5 us (5%)
  matrix products  11.8 us (5%)
  other arithmetic  6.5 us (3%)
  local copies, waits for them, and re-layouts  4.7 us (2%)
    all_gather x1, waiting for transfers between devices, gather_turned(): result = lax.all_gather(both, axis, axis=0, tiled=True)  146 us
    all_to_all x1, blocking collectives, sum_at_owner(): lax.all_to_all(in_blocks(value, dim, devices), axis, 0, 0, tiled=True)  76.6 us
    dot_general x1, matrix products, shards(): jnp.dot(placing, partial_terms, preferred_element_type=jnp.float32)  5.36 us
  transfers between devices with their start and end apart: 1, of which 1 were waited for; matrix products, arithmetic and copies ran while one was open for 2% of the time, Pallas kernels for 0%

commit v1 on v0

--- a/solution.py
+++ b/solution.py
@@ -8,7 +8,9 @@
     turned = [jnp.moveaxis(a, dim, 0) for a, dim in zip(arrays, dims)]
     widths = [t[0].size for t in turned]
     both = jnp.concatenate([t.reshape(-1, w) for t, w in zip(turned, widths)], axis=1)
-    result = lax.all_gather(both, axis, axis=0, tiled=True)
+    result = jnp.concatenate(
+        lax.all_to_all(jnp.stack([both] * lax.axis_size(axis)), axis, 0, 0), axis=0
+    )
     blocks = jnp.split(result, [sum(widths[:k]) for k in range(1, len(widths))], axis=1)
     return tuple(
         (

time: 259 us -> 532 us (2.05)
  the two profiles are of different devices: /device:TPU:16 before, /device:TPU:1 now
where the time goes in v1:
time: 532 us
  waiting for transfers between devices  409 us (77%)
  blocking collectives  77.8 us (15%)
  starting transfers between devices  19.5 us (4%)
  matrix products  11.8 us (2%)
  local copies, waits for them, and re-layouts  9.39 us (2%)
    all_to_all x1, waiting for transfers between devices, gather_turned(): lax.all_to_all(jnp.stack([both] * lax.axis_size(axis)), axis, 0, 0)  409 us
    all_to_all x1, blocking collectives, sum_at_owner(): lax.all_to_all(in_blocks(value, dim, devices), axis, 0, 0, tiled=True)  77.8 us
    all_to_all x1, starting transfers between devices, gather_turned(): lax.all_to_all(jnp.stack([both] * lax.axis_size(axis)), axis, 0, 0)  19.5 us
  transfers between devices with their start and end apart: 1, of which 1 were waited for; matrix products, arithmetic and copies ran while one was open for 1% of the time, Pallas kernels for 0%

profile of v1, /device:TPU:1, one launch (start us, length us, event | category | flops | bytes accessed | tf_op | source)
XLA Modules:
  0.0 531.6 jit_solution(3503778399082322326)
XLA Ops:
  0.0 0.0 copy-start
  0.0 1.2 pad_maximum_fusion
  1.2 4.7 stack.2
  5.9 0.0 copy-start.2
  5.9 19.5 %all-to-all-start = ((bf16[32,96,1536]{2,1,0:T(8,128)(2,1)}), bf16[32,96,1536]{2,1,0:T(8,128)(2,1)}, u32[]{:S(2)}, u32[]{:S(2)}) async-start(bf16[32,96,1536]{2,1,0:T(8,128)(2,1)} %stack.2), calls=%async_computation | async-start | bytes 18874368 | tf_op jit(solution)/shard_map/all_to_all | solution.py:12
  25.4 0.0 copy-done.2
  25.5 0.0 copy-done
  25.5 0.0 copy-start.3
  25.5 0.0 copy-start.4
  25.5 2.7 gather_fusion
  28.2 0.0 copy-done.3
  28.2 0.0 copy-done.4
  28.2 1.9 gather_fusion.1
  30.2 408.6 %all-to-all-done = bf16[32,96,1536]{2,1,0:T(8,128)(2,1)} async-done(((bf16[32,96,1536]{2,1,0:T(8,128)(2,1)}), bf16[32,96,1536]{2,1,0:T(8,128)(2,1)}, u32[]{:S(2)}, u32[]{:S(2)}) %all-to-all-start) | async-done | bytes 9437216 | tf_op jit(solution)/shard_map/all_to_all | solution.py:12
  438.8 0.0 copy-start.1
  438.8 3.5 fusion.4
  442.3 0.0 copy-done.1
  442.3 2.9 fusion.14
  445.2 5.4 %convolution_convert_fusion = bf16[512,3072]{1,0:T(8,128)(2,1)} fusion(bf16[256,512]{1,0:T(8,128)(2,1)S(1)} %fusion.14, bf16[3072,1536]{1,0:T(8,128)(2,1)} %bitcast.4, s32[256]{0:T(256)S(1)} %bitcast.12), kind=kOutput, calls=%fused_computation.2 | convolution fusion | flops 1612316672 | bytes 6554624 | tf_op jit(solution)/shard_map/dot_general | solution.py:52
  450.6 77.8 %all_to_all.10 = bf16[16,32,3072]{2,1,0:T(8,128)(2,1)} all-to-all(bf16[16,32,3072]{2,1,0:T(8,128)(2,1)} %bitcast.8), channel_id=1, replica_groups=mesh['edp'=32,'etp'=16] {'etp'}, dimensions={0} | all-to-all | bytes 6291456 | tf_op jit(solution)/shard_map/all_to_all | solution.py:30
  528.4 3.2 reduce_sum.22
  (5 shorter events, 0.0 us)
Async XLA Ops:
  0.0 25.5 %copy-start = (bf16[512,3072]{1,0:T(8,128)(2,1)S(1)}, bf16[512,3072]{1,0:T(8,128)(2,1)}, u32[]{:S(2)}) copy-start(bf16[512,3072]{1,0:T(8,128)(2,1)} %param.7) | copy-start | bytes 9437188
  5.9 19.6 %copy-start.2 = (s32[1,256]{1,0:T(1,128)S(1)}, s32[1,256]{1,0:T(1,128)}, u32[]{:S(2)}) copy-start(s32[1,256]{1,0:T(1,128)} %param.10) | copy-start | bytes 3076
  5.9 432.9 %all-to-all-start = ((bf16[32,96,1536]{2,1,0:T(8,128)(2,1)}), bf16[32,96,1536]{2,1,0:T(8,128)(2,1)}, u32[]{:S(2)}, u32[]{:S(2)}) async-start(bf16[32,96,1536]{2,1,0:T(8,128)(2,1)} %stack.2), calls=%async_computation | async-start | bytes 18874368 | tf_op jit(solution)/shard_map/all_to_all | solution.py:12
  25.5 2.7 copy-start.3
  25.5 2.7 copy-start.4
  438.8 3.5 copy-start.1
